TPU v7x, 32 devices: a whole 2x2x4 slice. The times are simulated.
32 devices in a mesh: dp: 16 (over z, y, x), seq: 2 (over core).
Axes of the slice: x: 2, y: 2, z: 4, core: 2. Of those that a mesh axis runs over, the one named last changes fastest.
Arguments:
- chains_in: bfloat16 [128, 160, 768], P(('dp', 'seq')), may hold values from -6 to 6
- lengths: int32 [128], P(('dp', 'seq')), may hold values from 95 to 160
- d_out: bfloat16 [128, 160, 768], P(('dp', 'seq')), may hold values from -6 to 6
- w_query: bfloat16 [768, 768], replicated, may hold values from -0.21875 to 0.21875
- b_query: float32 [768], replicated, may hold values from -3 to 3
- w_key: bfloat16 [768, 768], replicated, may hold values from -0.21875 to 0.21875
- w_value: bfloat16 [768, 768], replicated, may hold values from -0.21875 to 0.21875
- b_value: float32 [768], replicated, may hold values from -3 to 3
- w_output: bfloat16 [768, 768], replicated, may hold values from -2.5 to 2.5
- b_output: float32 [768], replicated, may hold values from -3 to 3
- gain_one: float32 [768], replicated, may hold values from 0.25 to 1.75
- shift_one: float32 [768], replicated, may hold values from -2 to 2
- w_inner: bfloat16 [768, 3072], replicated, may hold values from -0.21875 to 0.21875
- b_inner: float32 [3072], replicated, may hold values from -3 to 3
- w_outer: bfloat16 [3072, 768], replicated, may hold values from -0.109375 to 0.109375
- b_outer: float32 [768], replicated, may hold values from -3 to 3
- gain_two: float32 [768], replicated, may hold values from 0.25 to 1.75
- shift_two: float32 [768], replicated, may hold values from -2 to 2
Outputs:
- layer_out: bfloat16 [128, 160, 768], P(('dp', 'seq'))
- d_x: float32 [128, 160, 768], P(('dp', 'seq'))
- d_w_query: float32 [768, 768], replicated
- d_b_query: float32 [768], replicated
- d_w_key: float32 [768, 768], replicated
- d_w_value: float32 [768, 768], replicated
- d_b_value: float32 [768], replicated
- d_w_output: float32 [768, 768], replicated
- d_b_output: float32 [768], replicated
- d_gain_one: float32 [768], replicated
- d_shift_one: float32 [768], replicated
- d_w_inner: float32 [768, 3072], replicated
- d_b_inner: float32 [3072], replicated
- d_w_outer: float32 [3072, 768], replicated
- d_b_outer: float32 [768], replicated
- d_gain_two: float32 [768], replicated
- d_shift_two: float32 [768], replicated
Inputs may be any that keep to these rules, and one draw needn't show every extreme that they name: `lengths`: every chain fills more than half of its 160 positions.
All inputs are finite; a program needn't handle non-finite values.
Results may differ from a plain program's by a relative error of at most 0.015.
Values may be sent and summed in bfloat16 or wider, within the bound.
No kernel may reach another device: no remote copies, remote signals or barrier semaphores. Data moves between devices by JAX's collectives and lax.ppermute only.
A program may use at most 256 MiB of HBM per device.

v0:
```python
import jax
import jax.numpy as jnp
from jax import lax
from jax.sharding import PartitionSpec as P

H = 12
EPS = 1e-12


def norm_forward(h, gain, shift):
    centre = h - jnp.mean(h, -1, keepdims=True)
    scale = lax.rsqrt(jnp.mean(centre * centre, -1, keepdims=True) + EPS)
    unit = centre * scale
    return (unit * gain + shift, unit, scale)


def norm_backward(grad, unit, scale, gain):
    d_gain = jnp.sum(grad * unit, 0)
    d_shift = jnp.sum(grad, 0)
    inner = grad * gain
    d_h = scale * (
        inner
        - jnp.mean(inner, -1, keepdims=True)
        - unit * jnp.mean(inner * unit, -1, keepdims=True)
    )
    return (d_h, d_gain, d_shift)


def over_rows(left, right):
    return lax.dot_general(
        left, right, (((0,), (0,)), ((), ())), preferred_element_type=jnp.float32
    )


def times_trans(left, weight):
    return lax.dot_general(
        left, weight, (((1,), (1,)), ((), ())), preferred_element_type=jnp.float32
    )


def attn_scores(query, keys, live_keys):
    seqs, count, width = query.shape
    total = keys.shape[1]
    size = width // H
    q_heads = query.reshape(seqs, count, H, size)
    k_heads = keys.reshape(seqs, total, H, size)
    scores = (
        jnp.einsum("bqhe,bkhe->bhqk", q_heads, k_heads, preferred_element_type=jnp.float32) * 0.125
    )
    return jnp.where(live_keys[:, None, None, :], scores, -1000000000.0)


def packed(grads, count):
    flat = jnp.concatenate([g.reshape(-1) for g in grads])
    extra = -flat.shape[0] % count
    return flat.reshape(count, -1)


def unpacked(flat, grads):
    flat = flat.reshape(-1)
    pieces = []
    start = 0
    for grad in grads:
        number = grad.size
        pieces.append(flat[start : start + number].reshape(grad.shape))
        start = start + number
    return tuple(pieces)


def body(
    chains_in,
    lengths,
    d_out,
    w_query,
    b_query,
    w_key,
    w_value,
    b_value,
    w_output,
    b_output,
    gain_one,
    shift_one,
    w_inner,
    b_inner,
    w_outer,
    b_outer,
    gain_two,
    shift_two,
):
    f32 = jnp.float32
    low_type = jnp.bfloat16
    seqs, length, width = chains_in.shape
    rows = seqs * length
    size = width // H
    parts = lax.axis_size("dp")
    count = lax.axis_size("dp") * lax.axis_size("seq")
    place = jnp.arange(length, dtype=jnp.int32)
    live_rows = place[None, :] < lengths[:, None]
    flat_x = chains_in.reshape(rows, width)
    query = (
        (jnp.dot(flat_x, w_query, preferred_element_type=f32) + b_query)
        .astype(low_type)
        .reshape(seqs, length, width)
    )
    keys = (
        jnp.dot(flat_x, w_key, preferred_element_type=f32)
        .astype(low_type)
        .reshape(seqs, length, width)
    )
    values = (
        (jnp.dot(flat_x, w_value, preferred_element_type=f32) + b_value)
        .astype(low_type)
        .reshape(seqs, length, width)
    )
    scores = attn_scores(query, keys, live_rows)
    top = jnp.max(scores, -1, keepdims=True)
    expo = jnp.exp(scores - top)
    summed = jnp.sum(expo, -1, keepdims=True)
    prob_b = (expo / summed).astype(low_type)
    lse = top + jnp.log(summed)
    v_heads = values.reshape(seqs, length, H, size)
    mixed = (
        jnp.einsum("bhqk,bkhe->bqhe", prob_b, v_heads, preferred_element_type=f32)
        .reshape(rows, width)
        .astype(low_type)
    )
    h_one = flat_x.astype(f32) + jnp.dot(mixed, w_output, preferred_element_type=f32) + b_output
    first, unit_one, scale_one = norm_forward(h_one, gain_one, shift_one)
    live_flat = live_rows.reshape(rows)
    fin = first.astype(low_type)
    pre = jnp.dot(fin, w_inner, preferred_element_type=f32) + b_inner
    hidden = jax.nn.gelu(pre, approximate=False).astype(low_type)
    ffn_home = (jnp.dot(hidden, w_outer, preferred_element_type=f32) + b_outer).astype(low_type)
    h_two = first + ffn_home.astype(f32)
    second, unit_two, scale_two = norm_forward(h_two, gain_two, shift_two)
    keep = live_flat[:, None].astype(f32)
    layer_out = (second * keep).astype(low_type).reshape(seqs, length, width)
    grad_out = d_out.reshape(rows, width).astype(f32) * keep
    d_h_two, d_gain_two, d_shift_two = norm_backward(grad_out, unit_two, scale_two, gain_two)
    d_ffn = d_h_two.astype(low_type)
    d_w_outer = over_rows(hidden, d_ffn)
    d_b_outer = jnp.sum(d_ffn.astype(f32), 0)
    d_hidden = times_trans(d_ffn, w_outer)
    gelu_pull = jax.vjp(lambda z: jax.nn.gelu(z, approximate=False), pre)[1]
    d_pre = gelu_pull(d_hidden)[0].astype(low_type)
    d_w_inner = over_rows(fin, d_pre)
    d_b_inner = jnp.sum(d_pre.astype(f32), 0)
    d_fin = times_trans(d_pre, w_inner).astype(low_type)
    d_home = d_fin
    d_first = d_h_two + d_home.astype(f32)
    ffn_grads = (d_w_inner, d_b_inner, d_w_outer, d_b_outer, d_gain_two, d_shift_two)
    d_h_one, d_gain_one, d_shift_one = norm_backward(d_first, unit_one, scale_one, gain_one)
    d_attn = d_h_one.astype(low_type)
    d_w_output = over_rows(mixed, d_attn)
    d_b_output = jnp.sum(d_attn.astype(f32), 0)
    d_mixed = times_trans(d_attn, w_output).astype(low_type).reshape(seqs, length, H, size)
    scores = attn_scores(query, keys, live_rows)
    prob = jnp.exp(scores - lse)
    prob_b = prob.astype(low_type)
    d_prob = jnp.einsum("bqhe,bkhe->bhqk", d_mixed, v_heads, preferred_element_type=f32)
    delta = jnp.sum(prob * d_prob, -1, keepdims=True)
    d_scores = (prob * (d_prob - delta)).astype(low_type)
    k_heads = keys.reshape(seqs, length, H, size)
    q_heads = query.reshape(seqs, length, H, size)
    d_query = (
        (jnp.einsum("bhqk,bkhe->bqhe", d_scores, k_heads, preferred_element_type=f32) * 0.125)
        .astype(low_type)
        .reshape(rows, width)
    )
    d_key = (
        (jnp.einsum("bhqk,bqhe->bkhe", d_scores, q_heads, preferred_element_type=f32) * 0.125)
        .astype(low_type)
        .reshape(rows, width)
    )
    d_value = (
        jnp.einsum("bhqk,bqhe->bkhe", prob_b, d_mixed, preferred_element_type=f32)
        .astype(low_type)
        .reshape(rows, width)
    )
    d_w_query = over_rows(flat_x, d_query)
    d_b_query = jnp.sum(d_query.astype(f32), 0)
    d_w_key = over_rows(flat_x, d_key)
    d_w_value = over_rows(flat_x, d_value)
    d_b_value = jnp.sum(d_value.astype(f32), 0)
    d_x = (
        d_h_one
        + times_trans(d_query, w_query)
        + times_trans(d_key, w_key)
        + times_trans(d_value, w_value)
    )
    d_x = d_x.reshape(seqs, length, width)
    attn_grads = (
        d_w_query,
        d_b_query,
        d_w_key,
        d_w_value,
        d_b_value,
        d_w_output,
        d_b_output,
        d_gain_one,
        d_shift_one,
    )
    local_grads = attn_grads + ffn_grads
    big = [g for g in local_grads if g.ndim == 2]
    small = [g for g in local_grads if g.ndim == 1]
    sums = lax.psum(jnp.concatenate(small), ("dp", "seq"))
    small_sums = unpacked(sums, small)
    big_sums = []
    for grad in big:
        part = lax.psum_scatter(
            grad.astype(low_type), ("dp", "seq"), scatter_dimension=0, tiled=True
        )
        big_sums.append(lax.all_gather(part, ("dp", "seq"), axis=0, tiled=True).astype(f32))
    every = []
    for grad in local_grads:
        every.append(big_sums.pop(0) if grad.ndim == 2 else small_sums[0])
        small_sums = small_sums if grad.ndim == 2 else small_sums[1:]
    return (
        layer_out,
        d_x,
        every[0],
        every[1],
        every[2],
        every[3],
        every[4],
        every[5],
        every[6],
        every[7],
        every[8],
        every[9],
        every[10],
        every[11],
        every[12],
        every[13],
        every[14],
    )


def solution(mesh):
    return jax.shard_map(
        body,
        mesh=mesh,
        in_specs=(
            P(("dp", "seq"), None, None),
            P(("dp", "seq")),
            P(("dp", "seq"), None, None),
            P(),
            P(),
            P(),
            P(),
            P(),
            P(),
            P(),
            P(),
            P(),
            P(),
            P(),
            P(),
            P(),
            P(),
            P(),
        ),
        out_specs=(
            P(("dp", "seq"), None, None),
            P(("dp", "seq"), None, None),
            P(),
            P(),
            P(),
            P(),
            P(),
            P(),
            P(),
            P(),
            P(),
            P(),
            P(),
            P(),
            P(),
            P(),
            P(),
        ),
        check_vma=False,
    )
```

profile of v0, /device:TPU:0, one launch (start us, length us, event | category | flops | bytes accessed | tf_op | source)
XLA Modules:
  0.0 1139.7 jit_solution(12008616428699110538)
XLA Ops:
  12.5 4.6 copy.78
  22.2 4.5 copy.76
  47.0 4.1 convert_element_type.174
  55.6 23.9 %multiply_convert_fusion.1 = (bf16[640,3072]{1,0:T(8,128)(2,1)S(1)}, f32[640,3072]{1,0:T(8,128)}, f32[640,3072]{1,0:T(8,128)}) fusion(f32[3072]{0:T(1024)S(1)} %copy-done.22, bf16[768,3072]{1,0:T(8,128)(2,1)} %param.30, f32[640,768]{1,0:T(8,128)} %copy-done.8, f32[768]{0:T(1024)S(1)} %copy-done.26, f32[768]{0:T(1024)S(1)} %copy-done.19, ...), kind=kOutput, calls=%fused_computation.7 | convolution fusion | flops 3152117760 | bytes 26369024 | tf_op jit(solution)/shard_map/dot_general | solution.py:131
  79.5 7.2 fusion.47
  93.5 11.6 %convert_reduce_fusion = (f32[3072]{0:T(1024)S(1)}, bf16[640,3072]{1,0:T(8,128)(2,1)S(1)}) fusion(f32[640,3072]{1,0:T(8,128)} %get-tuple-element.64, bf16[3072,768]{1,0:T(8,128)(2,1)} %param.32, f32[640,768]{1,0:T(8,128)S(1)} %get-tuple-element.60, f32[640,3072]{1,0:T(8,128)} %get-tuple-element.80, f32[3072]{0:T(1024)S(1)} %copy-done.22), kind=kOutput, calls=%fused_computation.2 | convolution fusion | flops 3053810688 | bytes 26370048 | tf_op jit(solution)/shard_map/dot_general | solution.py:36
  105.2 3.8 multiply_reduce_fusion.2
  112.9 4.1 reshape.194
  117.0 4.6 copy.82
  121.6 7.5 multiply_reduce_fusion
  129.1 4.9 multiply_convert_fusion
  138.9 3.6 fusion.26
  151.6 3.6 fusion.27
  157.8 5.5 convert_reduce_fusion.1
  166.5 3.6 fusion.28
  176.2 9.1 convolution_convert_fusion.1
  185.3 8.8 convolution_convert_fusion
  194.3 49.8 %reduce-scatter.19.cloned.1.call-done = bf16[24,768]{1,0:T(8,128)(2,1)} async-done(((bf16[768,768]{1,0:T(8,128)(2,1)}), bf16[24,768]{1,0:T(8,128)(2,1)}) %reduce-scatter.19.cloned.1.call-update) | async-done | bytes 36880 | tf_op jit(solution)/shard_map/reduce_scatter | solution.py:210
  244.2 100.9 %reduce-scatter.21.cloned.1.call-done = bf16[24,768]{1,0:T(8,128)(2,1)} async-done(((bf16[768,768]{1,0:T(8,128)(2,1)}), bf16[24,768]{1,0:T(8,128)(2,1)}) %reduce-scatter.21.cloned.1.call-update) | async-done | bytes 36880 | tf_op jit(solution)/shard_map/reduce_scatter | solution.py:210
  345.1 100.4 %reduce-scatter.23.cloned.1.call-done = bf16[24,768]{1,0:T(8,128)(2,1)} async-done(((bf16[768,768]{1,0:T(8,128)(2,1)}), bf16[24,768]{1,0:T(8,128)(2,1)}) %reduce-scatter.23.cloned.1.call-update) | async-done | bytes 36880 | tf_op jit(solution)/shard_map/reduce_scatter | solution.py:210
  445.6 100.8 %reduce-scatter.13.cloned.1.call-done = bf16[24,768]{1,0:T(8,128)(2,1)} async-done(((bf16[768,768]{1,0:T(8,128)(2,1)}), bf16[24,768]{1,0:T(8,128)(2,1)}) %reduce-scatter.13.cloned.1.call-update) | async-done | bytes 36880 | tf_op jit(solution)/shard_map/reduce_scatter | solution.py:210
  546.4 111.9 %reduce-scatter.15.cloned.1.call-done = bf16[24,3072]{1,0:T(8,128)(2,1)} async-done(((bf16[768,3072]{1,0:T(8,128)(2,1)}), bf16[24,3072]{1,0:T(8,128)(2,1)}) %reduce-scatter.15.cloned.1.call-update) | async-done | bytes 147472 | tf_op jit(solution)/shard_map/reduce_scatter | solution.py:210
  658.4 112.9 %reduce-scatter.17.cloned.1.call-done = bf16[96,768]{1,0:T(8,128)(2,1)} async-done(((bf16[3072,768]{1,0:T(8,128)(2,1)}), bf16[96,768]{1,0:T(8,128)(2,1)}) %reduce-scatter.17.cloned.1.call-update) | async-done | bytes 147472 | tf_op jit(solution)/shard_map/reduce_scatter | solution.py:210
  771.5 40.6 %psum.7 = f32[9216]{0:T(1024)S(1)} all-reduce(f32[9216]{0:T(1024)S(1)} %constant_dynamic-update-slice_fusion), channel_id=1, replica_groups=mesh['dp'=16,'seq'=2] {'dp','seq'}, use_global_device_ids=true, to_apply=%region_21.22 | all-reduce | flops 9216 | bytes 73728 | tf_op jit(solution)/shard_map/psum | solution.py:206
  820.0 7.2 all-gather.7.cloned.1.call-done
  830.1 53.1 %all-gather.9.cloned.1.call-done = bf16[768,768]{1,0:T(8,128)(2,1)} async-done(((bf16[24,768]{1,0:T(8,128)(2,1)}), bf16[768,768]{1,0:T(8,128)(2,1)}) %all-gather.9.cloned.1.call-update) | async-done | bytes 1179664 | tf_op jit(solution)/shard_map/all_gather | solution.py:213
  886.0 53.1 %all-gather.11.cloned.1.call-done = bf16[768,768]{1,0:T(8,128)(2,1)} async-done(((bf16[24,768]{1,0:T(8,128)(2,1)}), bf16[768,768]{1,0:T(8,128)(2,1)}) %all-gather.11.cloned.1.call-update) | async-done | bytes 1179664 | tf_op jit(solution)/shard_map/all_gather | solution.py:213
  941.9 52.9 %all-gather.13.cloned.1.call-done = bf16[768,768]{1,0:T(8,128)(2,1)} async-done(((bf16[24,768]{1,0:T(8,128)(2,1)}), bf16[768,768]{1,0:T(8,128)(2,1)}) %all-gather.13.cloned.1.call-update) | async-done | bytes 1179664 | tf_op jit(solution)/shard_map/all_gather | solution.py:213
  997.7 62.7 %all-gather.15.cloned.1.call-done = bf16[768,3072]{1,0:T(8,128)(2,1)} async-done(((bf16[24,3072]{1,0:T(8,128)(2,1)}), bf16[768,3072]{1,0:T(8,128)(2,1)}) %all-gather.15.cloned.1.call-update) | async-done | bytes 4718608 | tf_op jit(solution)/shard_map/all_gather | solution.py:213
  1060.4 7.4 convert_element_type.217
  1067.7 57.9 %all-gather.17.cloned.1.call-done = bf16[3072,768]{1,0:T(8,128)(2,1)} async-done(((bf16[96,768]{1,0:T(8,128)(2,1)}), bf16[3072,768]{1,0:T(8,128)(2,1)}) %all-gather.17.cloned.1.call-update) | async-done | bytes 4718608 | tf_op jit(solution)/shard_map/all_gather | solution.py:213
  1125.6 6.8 convert_element_type.219
  (150 shorter events, 91.1 us)
Async XLA Ops:
  7.2 43.9 %copy-start = (bf16[768,768]{1,0:T(8,128)(2,1)S(1)}, bf16[768,768]{1,0:T(8,128)(2,1)}, u32[]{:S(2)}) copy-start(bf16[768,768]{1,0:T(8,128)(2,1)} %param.26) | copy-start | bytes 3538948
  7.2 236.9 %reduce-scatter.19.cloned.1.call-start = ((), (), s32[]{:S(2)}) async-start(), calls=%async_computation.15 | async-start | bytes 1216512 | tf_op jit(solution)/shard_map/reduce_scatter | solution.py:210
  12.5 4.6 copy-start.20
  12.5 4.6 copy-start.23
  39.0 3.2 copy-start.1
  44.6 6.5 copy-start.24
  51.1 4.4 copy-start.19
  51.1 4.4 copy-start.22
  51.1 4.4 copy-start.26
  55.5 24.0 %copy-start.9 = (f32[640,768]{1,0:T(8,128)S(1)}, f32[640,768]{1,0:T(8,128)}, u32[]{:S(2)}) copy-start(f32[640,768]{1,0:T(8,128)} %copy-done.8) | copy-start | bytes 5898244
  55.5 24.0 %copy-start.25 = (f32[768]{0:T(1024)S(1)}, f32[768]{0:T(1024)}, u32[]{:S(2)}) copy-start(f32[768]{0:T(1024)} %param.33) | copy-start | bytes 9220
  79.5 7.2 copy-start.27
  79.5 7.6 copy-start.17
  86.7 3.3 copy-start.3
  90.2 15.0 %slice-start = ((s8[4718592]{0:T(1024)(128)(4,1)}), s8[4194304]{0:T(1024)(128)(4,1)S(1)}, s32[]{:S(2)}) async-start(s8[4718592]{0:T(1024)(128)(4,1)} %bitcast.81), calls=%async_computation.18 | async-start | bytes 8388608
  93.5 11.7 %copy-start.14 = (f32[640,768]{1,0:T(8,128)}, f32[640,768]{1,0:T(8,128)S(1)}, u32[]{:S(2)}) copy-start(f32[640,768]{1,0:T(8,128)S(1)} %get-tuple-element.60) | copy-start | bytes 5898244
  93.5 11.7 %copy-start.10 = (f32[640,768]{1,0:T(8,128)S(1)}, f32[640,768]{1,0:T(8,128)}, u32[]{:S(2)}) copy-start(f32[640,768]{1,0:T(8,128)} %copy-done.8) | copy-start | bytes 5898244
  93.5 11.7 %slice-start.1 = ((s8[4718592]{0:T(1024)(128)(4,1)}), s8[524288]{0:T(1024)(128)(4,1)S(1)}, s32[]{:S(2)}) async-start(s8[4718592]{0:T(1024)(128)(4,1)} %bitcast.81), calls=%async_computation.19 | async-start | bytes 1048576
  105.1 3.9 copy-start.28
  145.0 200.0 %reduce-scatter.21.cloned.1.call-start = ((), (), s32[]{:S(2)}) async-start(), calls=%async_computation.16 | async-start | bytes 1216512 | tf_op jit(solution)/shard_map/reduce_scatter | solution.py:210
  157.7 287.8 %reduce-scatter.23.cloned.1.call-start = ((), (), s32[]{:S(2)}) async-start(), calls=%async_computation.17 | async-start | bytes 1216512 | tf_op jit(solution)/shard_map/reduce_scatter | solution.py:210
  172.7 373.6 %reduce-scatter.13.cloned.1.call-start = ((), (), s32[]{:S(2)}) async-start(), calls=%async_computation.9 | async-start | bytes 1216512 | tf_op jit(solution)/shard_map/reduce_scatter | solution.py:210
  176.1 482.2 %reduce-scatter.15.cloned.1.call-start = ((), (), s32[]{:S(2)}) async-start(), calls=%async_computation.11 | async-start | bytes 4866048 | tf_op jit(solution)/shard_map/reduce_scatter | solution.py:210
  185.3 585.9 %reduce-scatter.17.cloned.1.call-start = ((), (), s32[]{:S(2)}) async-start(), calls=%async_computation.13 | async-start | bytes 4866048 | tf_op jit(solution)/shard_map/reduce_scatter | solution.py:210
  194.2 633.1 %all-gather.7.cloned.1.call-start = ((), (), s32[]{:S(2)}) async-start(), calls=%async_computation.6 | async-start | bytes 1216512 | tf_op jit(solution)/shard_map/all_gather | solution.py:213
  244.1 639.1 %all-gather.9.cloned.1.call-start = ((), (), s32[]{:S(2)}) async-start(), calls=%async_computation.7 | async-start | bytes 1216512 | tf_op jit(solution)/shard_map/all_gather | solution.py:213
  345.0 594.0 %all-gather.11.cloned.1.call-start = ((), (), s32[]{:S(2)}) async-start(), calls=%async_computation.8 | async-start | bytes 1216512 | tf_op jit(solution)/shard_map/all_gather | solution.py:213
  445.5 549.3 %all-gather.13.cloned.1.call-start = ((), (), s32[]{:S(2)}) async-start(), calls=%async_computation.10 | async-start | bytes 1216512 | tf_op jit(solution)/shard_map/all_gather | solution.py:213
  546.3 514.0 %all-gather.15.cloned.1.call-start = ((), (), s32[]{:S(2)}) async-start(), calls=%async_computation.12 | async-start | bytes 4866048 | tf_op jit(solution)/shard_map/all_gather | solution.py:213
  658.3 467.3 %all-gather.17.cloned.1.call-start = ((), (), s32[]{:S(2)}) async-start(), calls=%async_computation.14 | async-start | bytes 4866048 | tf_op jit(solution)/shard_map/all_gather | solution.py:213
  812.7 3.4 copy-start.16
  812.7 3.4 copy-start.21
  (11 other events, 23.1 us)
Sparse Core Ops, SparseCore 0:
  145.2 98.8 reduce-scatter.18
  249.7 95.2 reduce-scatter.20
  350.1 95.3 reduce-scatter.22
  451.0 95.2 reduce-scatter.12
  552.2 106.0 reduce-scatter.14
  665.1 106.0 reduce-scatter.16
  774.1 53.1 all-gather.6
  830.2 52.9 all-gather.8
  886.1 52.9 all-gather.10
  941.8 52.9 all-gather.12
  997.7 62.5 all-gather.14
  1063.1 62.4 all-gather.16
where the time goes:
time: 1150 us; the launch traced here: 1140 us
  waiting for transfers between devices  864 us (75%)
  matrix products  120 us (10%)
  local copies, waits for them, and re-layouts  60.8 us (5%)
  blocking collectives  40.6 us (4%)
  other arithmetic  38.7 us (3%)
  between operations  15.3 us (1%)
    reduce_scatter x6, waiting for transfers between devices, body(): lax.psum_scatter(grad.astype(low_type), ('dp', 'seq'), scatter_dimension=...  577 us
    all_gather x6, waiting for transfers between devices, body(): lax.all_gather(part, ('dp', 'seq'), axis=0, tiled=True).astype(f32)  287 us
    psum x1, blocking collectives, body(): sums = lax.psum(jnp.concatenate(small), ('dp', 'seq'))  40.6 us
    dot_general x6, matrix products, over_rows(): lax.dot_general(left, right, (((0,), (0,)), ((), ())), preferred_element_...  32.1 us
    convert_element_type x6, other arithmetic, body(): lax.all_gather(part, ('dp', 'seq'), axis=0, tiled=True).astype(f32)  25.6 us
    dot_general x1, matrix products, body(): pre = jnp.dot(fin, w_inner, preferred_element_type=f32) + b_inner  23.9 us
    dot_general x6, matrix products, times_trans(): lax.dot_general(left, weight, (((1,), (1,)), ((), ())), preferred_element...  23.5 us
  transfers between devices with their start and end apart: 12, of which 12 were waited for; matrix products, arithmetic and copies ran while one was open for 7% of the time, Pallas kernels for 0%

commit v1 on v0

--- a/solution.py
+++ b/solution.py
@@ -203,7 +203,7 @@
     local_grads = attn_grads + ffn_grads
     big = [g for g in local_grads if g.ndim == 2]
     small = [g for g in local_grads if g.ndim == 1]
-    sums = lax.psum(jnp.concatenate(small), ("dp", "seq"))
+    sums = lax.psum(lax.psum(jnp.concatenate(small), "seq"), "dp")
     small_sums = unpacked(sums, small)
     big_sums = []
     for grad in big:

time: 1150 us -> 1150 us (level)
  blocking collectives: 40.6 us -> 78.9 us
  waiting for transfers between devices: 864 us -> 826 us
    psum x1 -> x2, blocking collectives: 40.6 us -> 78.9 us  [body(): sums = lax.psum(lax.psum(jnp.concatenate(small), 'seq'), 'dp')]
    all_gather x6, waiting for transfers between devices: 287 us -> 249 us  [body(): lax.all_gather(part, ('dp', 'seq'), axis=0, tiled=True).astype(f32)]
  transfers between devices with their start and end apart: 12 -> 12, of which waited for: 12 -> 11; matrix products, arithmetic and copies ran while one was open for 7% -> 7% of each run, Pallas kernels for 0% -> 0%
where the time goes in v1:
time: 1150 us; the launch traced here: 1140 us
  waiting for transfers between devices  826 us (72%)
  matrix products  120 us (10%)
  blocking collectives  78.9 us (7%)
  local copies, waits for them, and re-layouts  60.8 us (5%)
  other arithmetic  38.7 us (3%)
  between operations  15.3 us (1%)
    reduce_scatter x6, waiting for transfers between devices, body(): lax.psum_scatter(grad.astype(low_type), ('dp', 'seq'), scatter_dimension=...  577 us
    all_gather x6, waiting for transfers between devices, body(): lax.all_gather(part, ('dp', 'seq'), axis=0, tiled=True).astype(f32)  249 us
    psum x2, blocking collectives, body(): sums = lax.psum(lax.psum(jnp.concatenate(small), 'seq'), 'dp')  78.9 us
    dot_general x6, matrix products, over_rows(): lax.dot_general(left, right, (((0,), (0,)), ((), ())), preferred_element_...  32.1 us
    convert_element_type x6, other arithmetic, body(): lax.all_gather(part, ('dp', 'seq'), axis=0, tiled=True).astype(f32)  25.6 us
    dot_general x1, matrix products, body(): pre = jnp.dot(fin, w_inner, preferred_element_type=f32) + b_inner  23.9 us
    dot_general x6, matrix products, times_trans(): lax.dot_general(left, weight, (((1,), (1,)), ((), ())), preferred_element...  23.3 us
  transfers between devices with their start and end apart: 12, of which 11 were waited for; matrix products, arithmetic and copies ran while one was open for 7% of the time, Pallas kernels for 0%

profile of v1, /device:TPU:0, one launch (start us, length us, event | category | flops | bytes accessed | tf_op | source)
XLA Modules:
  0.0 1139.7 jit_solution(13884935066364132452)
XLA Ops:
  12.5 4.6 copy.78
  22.2 4.5 copy.76
  35.4 3.6 fusion.12
  47.0 4.1 convert_element_type.174
  55.5 23.9 %multiply_convert_fusion.1 = (bf16[640,3072]{1,0:T(8,128)(2,1)S(1)}, f32[640,3072]{1,0:T(8,128)}, f32[640,3072]{1,0:T(8,128)}) fusion(f32[3072]{0:T(1024)S(1)} %copy-done.22, bf16[768,3072]{1,0:T(8,128)(2,1)} %param.30, f32[640,768]{1,0:T(8,128)} %copy-done.8, f32[768]{0:T(1024)S(1)} %copy-done.26, f32[768]{0:T(1024)S(1)} %copy-done.19, ...), kind=kOutput, calls=%fused_computation.7 | convolution fusion | flops 3152117760 | bytes 26369024 | tf_op jit(solution)/shard_map/dot_general | solution.py:131
  79.5 7.2 fusion.47
  93.5 11.6 %convert_reduce_fusion = (f32[3072]{0:T(1024)S(1)}, bf16[640,3072]{1,0:T(8,128)(2,1)S(1)}) fusion(f32[640,3072]{1,0:T(8,128)} %get-tuple-element.64, bf16[3072,768]{1,0:T(8,128)(2,1)} %param.32, f32[640,768]{1,0:T(8,128)S(1)} %get-tuple-element.60, f32[640,3072]{1,0:T(8,128)} %get-tuple-element.80, f32[3072]{0:T(1024)S(1)} %copy-done.22), kind=kOutput, calls=%fused_computation.2 | convolution fusion | flops 3053810688 | bytes 26370048 | tf_op jit(solution)/shard_map/dot_general | solution.py:36
  105.2 3.8 multiply_reduce_fusion.2
  112.9 4.1 reshape.194
  117.0 4.6 copy.82
  121.6 7.5 multiply_reduce_fusion
  129.0 4.9 multiply_convert_fusion
  138.9 3.6 fusion.26
  151.6 3.6 fusion.27
  157.8 5.5 convert_reduce_fusion.1
  166.5 3.6 fusion.28
  176.1 9.1 convolution_convert_fusion.1
  185.3 8.8 convolution_convert_fusion
  194.2 49.8 %reduce-scatter.19.cloned.1.call-done = bf16[24,768]{1,0:T(8,128)(2,1)} async-done(((bf16[768,768]{1,0:T(8,128)(2,1)}), bf16[24,768]{1,0:T(8,128)(2,1)}) %reduce-scatter.19.cloned.1.call-update) | async-done | bytes 36880 | tf_op jit(solution)/shard_map/reduce_scatter | solution.py:210
  244.1 100.9 %reduce-scatter.21.cloned.1.call-done = bf16[24,768]{1,0:T(8,128)(2,1)} async-done(((bf16[768,768]{1,0:T(8,128)(2,1)}), bf16[24,768]{1,0:T(8,128)(2,1)}) %reduce-scatter.21.cloned.1.call-update) | async-done | bytes 36880 | tf_op jit(solution)/shard_map/reduce_scatter | solution.py:210
  345.1 100.4 %reduce-scatter.23.cloned.1.call-done = bf16[24,768]{1,0:T(8,128)(2,1)} async-done(((bf16[768,768]{1,0:T(8,128)(2,1)}), bf16[24,768]{1,0:T(8,128)(2,1)}) %reduce-scatter.23.cloned.1.call-update) | async-done | bytes 36880 | tf_op jit(solution)/shard_map/reduce_scatter | solution.py:210
  445.5 100.8 %reduce-scatter.13.cloned.1.call-done = bf16[24,768]{1,0:T(8,128)(2,1)} async-done(((bf16[768,768]{1,0:T(8,128)(2,1)}), bf16[24,768]{1,0:T(8,128)(2,1)}) %reduce-scatter.13.cloned.1.call-update) | async-done | bytes 36880 | tf_op jit(solution)/shard_map/reduce_scatter | solution.py:210
  546.3 111.9 %reduce-scatter.15.cloned.1.call-done = bf16[24,3072]{1,0:T(8,128)(2,1)} async-done(((bf16[768,3072]{1,0:T(8,128)(2,1)}), bf16[24,3072]{1,0:T(8,128)(2,1)}) %reduce-scatter.15.cloned.1.call-update) | async-done | bytes 147472 | tf_op jit(solution)/shard_map/reduce_scatter | solution.py:210
  658.3 112.9 %reduce-scatter.17.cloned.1.call-done = bf16[96,768]{1,0:T(8,128)(2,1)} async-done(((bf16[3072,768]{1,0:T(8,128)(2,1)}), bf16[96,768]{1,0:T(8,128)(2,1)}) %reduce-scatter.17.cloned.1.call-update) | async-done | bytes 147472 | tf_op jit(solution)/shard_map/reduce_scatter | solution.py:210
  774.9 75.4 %psum.15 = f32[9216]{0:T(1024)S(1)} all-reduce(f32[9216]{0:T(1024)S(1)} %psum.14), channel_id=1, replica_groups=mesh['dp'=16,'seq'=2] {'dp'}, use_global_device_ids=true, to_apply=%region_22.23 | all-reduce | flops 9216 | bytes 73728 | tf_op jit(solution)/shard_map/psum | solution.py:206
  860.9 22.3 %all-gather.9.cloned.1.call-done = bf16[768,768]{1,0:T(8,128)(2,1)} async-done(((bf16[24,768]{1,0:T(8,128)(2,1)}), bf16[768,768]{1,0:T(8,128)(2,1)}) %all-gather.9.cloned.1.call-update) | async-done | bytes 1179664 | tf_op jit(solution)/shard_map/all_gather | solution.py:213
  886.0 53.1 %all-gather.11.cloned.1.call-done = bf16[768,768]{1,0:T(8,128)(2,1)} async-done(((bf16[24,768]{1,0:T(8,128)(2,1)}), bf16[768,768]{1,0:T(8,128)(2,1)}) %all-gather.11.cloned.1.call-update) | async-done | bytes 1179664 | tf_op jit(solution)/shard_map/all_gather | solution.py:213
  942.0 52.9 %all-gather.13.cloned.1.call-done = bf16[768,768]{1,0:T(8,128)(2,1)} async-done(((bf16[24,768]{1,0:T(8,128)(2,1)}), bf16[768,768]{1,0:T(8,128)(2,1)}) %all-gather.13.cloned.1.call-update) | async-done | bytes 1179664 | tf_op jit(solution)/shard_map/all_gather | solution.py:213
  997.7 62.7 %all-gather.15.cloned.1.call-done = bf16[768,3072]{1,0:T(8,128)(2,1)} async-done(((bf16[24,3072]{1,0:T(8,128)(2,1)}), bf16[768,3072]{1,0:T(8,128)(2,1)}) %all-gather.15.cloned.1.call-update) | async-done | bytes 4718608 | tf_op jit(solution)/shard_map/all_gather | solution.py:213
  1060.4 7.4 convert_element_type.217
  1067.7 57.9 %all-gather.17.cloned.1.call-done = bf16[3072,768]{1,0:T(8,128)(2,1)} async-done(((bf16[96,768]{1,0:T(8,128)(2,1)}), bf16[3072,768]{1,0:T(8,128)(2,1)}) %all-gather.17.cloned.1.call-update) | async-done | bytes 4718608 | tf_op jit(solution)/shard_map/all_gather | solution.py:213
  1125.6 6.8 convert_element_type.219
  (151 shorter events, 90.9 us)
Async XLA Ops:
  7.2 43.9 %copy-start = (bf16[768,768]{1,0:T(8,128)(2,1)S(1)}, bf16[768,768]{1,0:T(8,128)(2,1)}, u32[]{:S(2)}) copy-start(bf16[768,768]{1,0:T(8,128)(2,1)} %param.26) | copy-start | bytes 3538948
  7.2 236.8 %reduce-scatter.19.cloned.1.call-start = ((), (), s32[]{:S(2)}) async-start(), calls=%async_computation.15 | async-start | bytes 1216512 | tf_op jit(solution)/shard_map/reduce_scatter | solution.py:210
  12.5 4.6 copy-start.20
  12.5 4.6 copy-start.23
  39.0 3.2 copy-start.1
  44.6 6.5 copy-start.24
  51.1 4.4 copy-start.19
  51.1 4.4 copy-start.22
  51.1 4.4 copy-start.26
  55.5 24.0 %copy-start.9 = (f32[640,768]{1,0:T(8,128)S(1)}, f32[640,768]{1,0:T(8,128)}, u32[]{:S(2)}) copy-start(f32[640,768]{1,0:T(8,128)} %copy-done.8) | copy-start | bytes 5898244
  55.5 24.0 %copy-start.25 = (f32[768]{0:T(1024)S(1)}, f32[768]{0:T(1024)}, u32[]{:S(2)}) copy-start(f32[768]{0:T(1024)} %param.33) | copy-start | bytes 9220
  79.5 7.2 copy-start.27
  79.5 7.6 copy-start.17
  86.7 3.3 copy-start.3
  90.1 15.0 %slice-start = ((s8[4718592]{0:T(1024)(128)(4,1)}), s8[4194304]{0:T(1024)(128)(4,1)S(1)}, s32[]{:S(2)}) async-start(s8[4718592]{0:T(1024)(128)(4,1)} %bitcast.81), calls=%async_computation.18 | async-start | bytes 8388608
  93.5 11.7 %copy-start.14 = (f32[640,768]{1,0:T(8,128)}, f32[640,768]{1,0:T(8,128)S(1)}, u32[]{:S(2)}) copy-start(f32[640,768]{1,0:T(8,128)S(1)} %get-tuple-element.60) | copy-start | bytes 5898244
  93.5 11.7 %copy-start.10 = (f32[640,768]{1,0:T(8,128)S(1)}, f32[640,768]{1,0:T(8,128)}, u32[]{:S(2)}) copy-start(f32[640,768]{1,0:T(8,128)} %copy-done.8) | copy-start | bytes 5898244
  93.5 11.7 %slice-start.1 = ((s8[4718592]{0:T(1024)(128)(4,1)}), s8[524288]{0:T(1024)(128)(4,1)S(1)}, s32[]{:S(2)}) async-start(s8[4718592]{0:T(1024)(128)(4,1)} %bitcast.81), calls=%async_computation.19 | async-start | bytes 1048576
  105.1 3.9 copy-start.28
  145.0 200.0 %reduce-scatter.21.cloned.1.call-start = ((), (), s32[]{:S(2)}) async-start(), calls=%async_computation.16 | async-start | bytes 1216512 | tf_op jit(solution)/shard_map/reduce_scatter | solution.py:210
  157.7 287.7 %reduce-scatter.23.cloned.1.call-start = ((), (), s32[]{:S(2)}) async-start(), calls=%async_computation.17 | async-start | bytes 1216512 | tf_op jit(solution)/shard_map/reduce_scatter | solution.py:210
  172.7 373.6 %reduce-scatter.13.cloned.1.call-start = ((), (), s32[]{:S(2)}) async-start(), calls=%async_computation.9 | async-start | bytes 1216512 | tf_op jit(solution)/shard_map/reduce_scatter | solution.py:210
  176.1 482.2 %reduce-scatter.15.cloned.1.call-start = ((), (), s32[]{:S(2)}) async-start(), calls=%async_computation.11 | async-start | bytes 4866048 | tf_op jit(solution)/shard_map/reduce_scatter | solution.py:210
  185.3 585.9 %reduce-scatter.17.cloned.1.call-start = ((), (), s32[]{:S(2)}) async-start(), calls=%async_computation.13 | async-start | bytes 4866048 | tf_op jit(solution)/shard_map/reduce_scatter | solution.py:210
  194.2 663.9 %all-gather.7.cloned.1.call-start = ((), (), s32[]{:S(2)}) async-start(), calls=%async_computation.6 | async-start | bytes 1216512 | tf_op jit(solution)/shard_map/all_gather | solution.py:213
  244.1 639.1 %all-gather.9.cloned.1.call-start = ((), (), s32[]{:S(2)}) async-start(), calls=%async_computation.7 | async-start | bytes 1216512 | tf_op jit(solution)/shard_map/all_gather | solution.py:213
  345.0 594.1 %all-gather.11.cloned.1.call-start = ((), (), s32[]{:S(2)}) async-start(), calls=%async_computation.8 | async-start | bytes 1216512 | tf_op jit(solution)/shard_map/all_gather | solution.py:213
  445.5 549.4 %all-gather.13.cloned.1.call-start = ((), (), s32[]{:S(2)}) async-start(), calls=%async_computation.10 | async-start | bytes 1216512 | tf_op jit(solution)/shard_map/all_gather | solution.py:213
  546.3 514.1 %all-gather.15.cloned.1.call-start = ((), (), s32[]{:S(2)}) async-start(), calls=%async_computation.12 | async-start | bytes 4866048 | tf_op jit(solution)/shard_map/all_gather | solution.py:213
  658.3 467.3 %all-gather.17.cloned.1.call-start = ((), (), s32[]{:S(2)}) async-start(), calls=%async_computation.14 | async-start | bytes 4866048 | tf_op jit(solution)/shard_map/all_gather | solution.py:213
  851.0 3.2 copy-start.16
  851.0 3.2 copy-start.21
  (11 other events, 23.1 us)
Sparse Core Ops, SparseCore 0:
  145.1 98.8 reduce-scatter.18
  249.7 95.2 reduce-scatter.20
  350.1 95.3 reduce-scatter.22
  451.0 95.2 reduce-scatter.12
  552.2 106.0 reduce-scatter.14
  665.1 106.0 reduce-scatter.16
  774.1 53.2 all-gather.6
  830.3 52.9 all-gather.8
  886.1 52.9 all-gather.10
  941.9 52.9 all-gather.12
  997.8 62.5 all-gather.14
  1063.1 62.4 all-gather.16
